TPU v7x, 32 devices: a whole 2x2x4 slice. The times are simulated.
32 devices in a mesh: dp: 4 (over y, x), tp: 8 (over z, core).
Axes of the slice: x: 2, y: 2, z: 4, core: 2. Of those that a mesh axis runs over, the one named last changes fastest.
Arguments:
- gradients: bfloat16 [4, 4, 3072, 768], P('dp', None, 'tp'), may hold values from -6 to 6, as said below
- right_factor: float32 [4, 768, 8], replicated, may hold values from -6 to 6
- weights_before: float32 [4, 3072, 768], P(None, 'tp', 'dp'), may hold values from -0.21875 to 0.21875
- momentum: float32 [4, 3072, 768], P(None, 'tp', 'dp'), may hold values from -0.3125 to 0.3125
Outputs:
- new_weights: float32 [4, 3072, 768], P(None, 'tp', 'dp')
- new_basis: float32 [4, 768, 8], replicated
- new_momentum: float32 [4, 3072, 768], P(None, 'tp', 'dp')
Inputs may be any that keep to these rules, and one draw needn't show every extreme that they name: gradients holds numbers from -6 to 6.
All inputs are finite; a program needn't handle non-finite values.
Results may differ from a plain program's by a relative error of at most 0.0003.
Values sent between devices are 32-bit elements.
A program may use at most 64 MiB of HBM per device.

v0:
```python
import jax
import jax.numpy as jnp
from jax import lax
from jax.sharding import PartitionSpec as P

RANK = 8


def on_device(gradients, right_factor, weights_before, momentum):
    own_grads = gradients[0]
    part_left = jnp.einsum(
        "liw,lwr->lir",
        own_grads,
        right_factor.astype(jnp.bfloat16),
        preferred_element_type=jnp.float32,
    )
    left = lax.psum(part_left, "dp")
    part_gram = jnp.einsum("lir,lis->lrs", left, left, precision=lax.Precision.HIGHEST)
    small_left = left.astype(jnp.bfloat16)
    part_right = jnp.einsum(
        "liw,lir->lwr", own_grads, small_left, preferred_element_type=jnp.float32
    )
    own_share = part_gram / lax.axis_size("dp")
    right, gram = lax.psum((part_right, own_share), ("dp", "tp"))
    gram = gram + 0.001 * jnp.mean(jnp.diagonal(gram, axis1=1, axis2=2), axis=1)[
        :, None, None
    ] * jnp.eye(RANK, dtype=jnp.float32)
    place = lax.axis_index("dp") * weights_before.shape[2]
    own_right = lax.dynamic_slice_in_dim(right, place, weights_before.shape[2], axis=1)
    root = jnp.linalg.cholesky(gram)
    half = lax.linalg.triangular_solve(
        root, jnp.swapaxes(own_right, 1, 2), left_side=True, lower=True
    )
    mixed = lax.linalg.triangular_solve(root, half, left_side=True, lower=True, transpose_a=True)
    change = jnp.einsum(
        "lir,lrw->liw", left, mixed, precision=lax.Precision.HIGHEST
    ) / lax.axis_size("dp")
    new_momentum = 0.9 * momentum + change
    new_weights = weights_before - 0.02 * new_momentum
    new_basis = right * lax.rsqrt(jnp.mean(right * right, axis=(1, 2), keepdims=True) + 1e-12)
    return (new_weights, new_basis, new_momentum)


def solution(mesh):
    in_specs = (P("dp", None, "tp", None), P(), P(None, "tp", "dp"), P(None, "tp", "dp"))
    out_specs = (P(None, "tp", "dp"), P(), P(None, "tp", "dp"))
    return jax.shard_map(
        on_device, mesh=mesh, in_specs=in_specs, out_specs=out_specs, check_vma=False
    )
```

profile of v0, /device:TPU:0, one launch (start us, length us, event | category | flops | bytes accessed | tf_op | source)
XLA Modules:
  0.0 171.1 jit_solution(5481928536512770521)
XLA Ops:
  7.2 0.0 copy-start
  7.2 0.0 all-reduce.2.cloned.1.call-start
  7.2 1.6 copy-done
  8.8 1.6 fusion.2
  10.4 18.2 %psum.21 = f32[4,384,8]{1,2,0:T(8,128)S(1)} all-reduce(f32[4,384,8]{1,2,0:T(8,128)S(1)} %fusion.2), channel_id=1, replica_groups=mesh['dp'=4,'tp'=8] {'dp'}, use_global_device_ids=true, to_apply=%region_0.0 | all-reduce | flops 12288 | bytes 98304 | tf_op jit(solution)/shard_map/psum | solution.py:17
  28.6 1.1 fusion.5
  29.7 0.0 all-reduce.2.cloned.1.call-update
  29.8 0.2 convolution_multiply_fusion.1
  30.0 0.1 copy.13
  30.0 39.5 %psum.22 = f32[4,8,8]{1,2,0:T(8,128)S(1)} all-reduce(f32[4,8,8]{1,2,0:T(8,128)S(1)} %convolution_multiply_fusion.1), channel_id=1, replica_groups=mesh['dp'=4,'tp'=8] {'dp','tp'}, use_global_device_ids=true, to_apply=%region_1.0 | all-reduce | flops 256 | bytes 2048 | tf_op jit(solution)/shard_map/psum | solution.py:24
  69.6 0.1 copy.12
  69.7 0.6 gather_fusion
  70.3 0.1 multiply_add_fusion
  70.4 0.1 copy.14
  70.4 0.1 fusion.15
  70.5 2.9 %custom-call.9 = f32[4,8,8]{2,1,0:T(8,128)S(1)} custom-call(f32[4,8,8]{2,1,0:T(8,128)S(1)} %fusion.15), custom_call_target="Cholesky" | custom-call | tf_op jit(solution)/shard_map/jit(cholesky)/cholesky | solution.py:30
  73.4 0.1 select_reduce_fusion
  73.5 0.1 compare_reduce_fusion
  73.6 0.1 select_bitcast_fusion
  73.7 2.5 %custom-call.10 = f32[4,1,8,8]{2,3,1,0:T(8,128)S(1)} custom-call(f32[4,1,8,8]{3,2,1,0:T(8,128)S(1)} %select_bitcast_fusion), custom_call_target="InvertDiagBlocksLowerTriangular" | custom-call | tf_op jit(solution)/shard_map/triangular_solve | solution.py:34
  76.2 80.7 %all-reduce.2.cloned.1.call-done = f32[4,768,8]{1,2,0:T(8,128)} async-done(((f32[4,768,8]{1,2,0:T(8,128)}), f32[4,768,8]{1,2,0:T(8,128)}) %all-reduce.2.cloned.1.call-update) | async-done | bytes 98320 | tf_op jit(solution)/shard_map/psum | solution.py:24
  156.9 1.0 multiply_reduce_fusion
  157.9 1.1 fusion.9
  159.0 0.2 fusion.12
  159.1 0.0 copy-start.1
  159.1 4.4 %multiply_subtract_fusion = (f32[4,384,192]{1,2,0:T(8,128)}, f32[4,384,192]{1,2,0:T(8,128)}) fusion(f32[4,384,192]{1,2,0:T(8,128)} %param.6, f32[4,384,8]{1,2,0:T(8,128)S(1)} %psum.21, f32[4,8,192]{2,1,0:T(8,128)S(1)} %fusion.12, f32[4,384,192]{1,2,0:T(8,128)} %param.7), kind=kOutput, calls=%fused_computation.7 | convolution fusion | flops 29786112 | bytes 4792320 | tf_op jit(solution)/shard_map/lir,lrw->liw/dot_general | solution.py:35
  163.5 0.0 copy-done.1
  163.5 0.7 broadcast_multiply_fusion
  (7 shorter events, 0.1 us)
Async XLA Ops:
  7.2 1.7 copy-start
  7.2 149.7 %all-reduce.2.cloned.1.call-start = ((), (), s32[]{:S(2)}) async-start(), calls=%async_computation | async-start | bytes 196608 | tf_op jit(solution)/shard_map/psum | solution.py:24
  159.1 4.4 %copy-start.1 = (f32[4,768,8]{1,2,0:T(8,128)S(1)}, f32[4,768,8]{1,2,0:T(8,128)}, u32[]{:S(2)}) copy-start(f32[4,768,8]{1,2,0:T(8,128)} %all-reduce.2.cloned.1.call-done) | copy-start | bytes 294916
Sparse Core Ops, SparseCore 0:
  29.8 126.9 all-reduce.1
where the time goes:
time: 171 us
  waiting for transfers between devices  80.7 us (47%)
  blocking collectives  57.7 us (34%)
  between operations  14.1 us (8%)
  matrix products  8.45 us (5%)
  other arithmetic  7.59 us (4%)
  local copies, waits for them, and re-layouts  2.47 us (1%)
    psum x1, waiting for transfers between devices, on_device(): right, gram = lax.psum((part_right, own_share), ('dp', 'tp'))  80.7 us
    psum x1, blocking collectives, on_device(): right, gram = lax.psum((part_right, own_share), ('dp', 'tp'))  39.5 us
    psum x1, blocking collectives, on_device(): left = lax.psum(part_left, 'dp')  18.2 us
    dot_general x1, matrix products, on_device(): jnp.einsum('lir,lrw->liw', left, mixed, precision=lax.Precision.HIGHEST)  4.38 us
  transfers between devices with their start and end apart: 1, of which 1 were waited for; matrix products, arithmetic and copies ran while one was open for 4% of the time, Pallas kernels for 0%

commit v1 on v0

v1 whole, which is shorter than its diff:
```python
import functools

import jax
import jax.numpy as jnp
from jax import lax
from jax.experimental import pallas as pl
from jax.experimental.pallas import tpu as pltpu
from jax.sharding import PartitionSpec as P

MESH = pl.DeviceIdType.MESH
LANES = 128


def split3(x):
    high = x.astype(jnp.bfloat16).astype(jnp.float32)
    rest = x - high
    mid = rest.astype(jnp.bfloat16).astype(jnp.float32)
    low = (rest - mid).astype(jnp.bfloat16).astype(jnp.float32)
    return high, mid, low


def kernel(
    ndp, ntp, grads, basis, weights, momentum,
    out_weights, out_basis, out_momentum,
    g_buf, w_buf, m_buf, lefts, grams, rights, parts, full, y_buf,
    g_sem, wm_sem, left_send, left_recv, gram_send, gram_recv, part_send, part_recv, full_send, full_recv,
):
    layers, rank, rows = lefts.shape[0], lefts.shape[2], lefts.shape[3]
    width = grads.shape[2]
    columns = weights.shape[1]
    n = ndp * ntp
    tiles = width // LANES
    pieces = layers * tiles
    my_dp, my_tp = lax.axis_index("dp"), lax.axis_index("tp")
    me = my_dp * ntp + my_tp

    def device(flat):
        return (flat // ntp, lax.rem(flat, ntp))

    loads = [pltpu.make_async_copy(grads.at[l], g_buf.at[l], g_sem.at[l]) for l in range(layers)]
    for load in loads:
        load.start()
    state_loads = [
        pltpu.make_async_copy(weights, w_buf, wm_sem.at[0]),
        pltpu.make_async_copy(momentum, m_buf, wm_sem.at[1]),
    ]
    for load in state_loads:
        load.start()

    grams[my_tp] = jnp.zeros(grams.shape[1:], jnp.float32)
    barrier = pltpu.get_barrier_semaphore()
    for k in range(1, n):
        pl.semaphore_signal(barrier, inc=1, device_id=device(lax.rem(me + k, n)), device_id_type=MESH)

    def left_copy(l, k):
        return pltpu.make_async_remote_copy(
            src_ref=lefts.at[l, my_dp], dst_ref=lefts.at[l, my_dp],
            send_sem=left_send, recv_sem=left_recv.at[l],
            device_id=(lax.rem(my_dp + k, ndp), my_tp), device_id_type=MESH,
        )

    for l in range(layers):
        loads[l].wait()
        lefts[l, my_dp] = lax.dot_general(
            basis[l], g_buf[l], (((1,), (1,)), ((), ())), preferred_element_type=jnp.float32
        )
        if l == 0:
            pl.semaphore_wait(barrier, n - 1)
        for k in range(1, ndp):
            left_copy(l, k).start()

    def part_copy(j):
        owner = j % n
        return pltpu.make_async_remote_copy(
            src_ref=rights.at[j], dst_ref=parts.at[j // n, me],
            send_sem=part_send, recv_sem=part_recv.at[j // n],
            device_id=(owner // ntp, owner % ntp), device_id_type=MESH,
        )

    all_left = []
    for l in range(layers):
        if ndp > 1:
            landed = lefts.at[l, pl.ds(0, ndp - 1)]
            pltpu.make_async_copy(landed, landed, left_recv.at[l]).wait()
        left = lefts[l, 0]
        for d in range(1, ndp):
            left = left + lefts[l, d]
        all_left.append(left)
        right = jnp.dot(left.astype(jnp.bfloat16), g_buf[l], preferred_element_type=jnp.float32)
        for t in range(tiles):
            rights[l * tiles + t] = right[:, t * LANES:(t + 1) * LANES]
        for t in range(tiles):
            j = l * tiles + t

            @pl.when(me != j % n)
            def _():
                part_copy(j).start()

    stacked = jnp.concatenate(all_left, axis=0)
    products = lax.dot_general(
        stacked, stacked, (((1,), (1,)), ((), ())),
        precision=lax.Precision.HIGHEST, preferred_element_type=jnp.float32,
    )
    where = lax.broadcasted_iota(jnp.int32, (rank, layers * rank), 1) // rank
    packed = jnp.zeros((rank, layers * rank), jnp.float32)
    for l in range(layers):
        packed = jnp.where(where == l, products[l * rank:(l + 1) * rank], packed)
    grams[my_tp, :, :layers * rank] = packed

    def gram_copy(k):
        return pltpu.make_async_remote_copy(
            src_ref=grams.at[my_tp], dst_ref=grams.at[my_tp],
            send_sem=gram_send, recv_sem=gram_recv,
            device_id=(my_dp, lax.rem(my_tp + k, ntp)), device_id_type=MESH,
        )

    for k in range(1, ntp):
        gram_copy(k).start()

    def full_copy(j, k):
        return pltpu.make_async_remote_copy(
            src_ref=full.at[j], dst_ref=full.at[j],
            send_sem=full_send, recv_sem=full_recv.at[j],
            device_id=device(lax.rem(me + k, n)), device_id_type=MESH,
        )

    for j in range(pieces):
        q = j // n

        @pl.when(me == j % n)
        def _():
            landed = parts.at[q, pl.ds(0, n - 1)]
            pltpu.make_async_copy(landed, landed, part_recv.at[q]).wait()
            parts[q, me] = rights[j]
            full[j] = jnp.sum(parts[q], axis=0)
            for k in range(1, n):
                full_copy(j, k).start()

    if ntp > 1:
        landed = grams.at[pl.ds(0, ntp - 1)]
        pltpu.make_async_copy(landed, landed, gram_recv).wait()
    gram_sum = jnp.sum(grams[...], axis=0)
    line = lax.broadcasted_iota(jnp.int32, (rank, rank), 0)
    diagonal = line == lax.broadcasted_iota(jnp.int32, (rank, rank), 1)
    step_line = lax.broadcasted_iota(jnp.int32, (rank, 1), 0)
    systems = []
    for l in range(layers):
        gram = gram_sum[:, l * rank:(l + 1) * rank]
        ridge = 0.001 * (jnp.sum(jnp.where(diagonal, gram, 0.0)) / rank)
        systems.append((gram + jnp.where(diagonal, ridge, 0.0), all_left[l]))
    for k in range(rank):
        after = []
        for gram, y in systems:
            pivot = 1.0 / gram[k:k + 1, k:k + 1]
            gram_row, y_row = gram[k:k + 1] * pivot, y[k:k + 1] * pivot
            factor = gram[:, k:k + 1]
            here = step_line == k
            after.append((
                jnp.where(here, gram_row, gram - factor * gram_row),
                jnp.where(here, y_row, y - factor * y_row),
            ))
        systems = after
    for l in range(layers):
        high, mid, low = split3(systems[l][1])
        y = jnp.concatenate([high, high, high, mid, mid, low], axis=0)
        y_buf[l] = y.astype(jnp.bfloat16)
    for load in state_loads:
        load.wait()

    shift = lax.rem(width - my_dp * columns, width)
    for l in range(layers):
        for t in range(tiles):
            j = l * tiles + t

            @pl.when(me != j % n)
            def _():
                pltpu.make_async_copy(full.at[j], full.at[j], full_recv.at[j]).wait()
        right = jnp.concatenate([full[l * tiles + t] for t in range(tiles)], axis=1)
        own = pltpu.roll(right, shift, 1)[:, :columns]
        high, mid, low = split3(own)
        own = jnp.concatenate([high, mid, low, high, mid, high], axis=0).T.astype(jnp.bfloat16)
        change = jnp.dot(own, y_buf[l], preferred_element_type=jnp.float32) / ndp
        moved = 0.9 * m_buf[l] + change
        out_momentum[l] = moved
        out_weights[l] = w_buf[l] - 0.02 * moved
        out_basis[l] = right * lax.rsqrt(jnp.mean(right * right) + 1e-12)

    for l in range(layers):
        for k in range(1, ndp):
            left_copy(l, k).wait_send()
    for k in range(1, ntp):
        gram_copy(k).wait_send()
    for j in range(pieces):

        @pl.when(me != j % n)
        def _():
            part_copy(j).wait_send()

        @pl.when(me == j % n)
        def _():
            for k in range(1, n):
                full_copy(j, k).wait_send()


def solution(mesh):
    ndp, ntp = mesh.shape["dp"], mesh.shape["tp"]
    n = ndp * ntp

    def on_device(gradients, right_factor, weights_before, momentum):
        layers, rows, width = gradients.shape[1:]
        rank = right_factor.shape[2]
        columns = weights_before.shape[2]
        pieces = layers * (width // LANES)
        rounds = -(-pieces // n)
        basis = jnp.swapaxes(right_factor, 1, 2).astype(jnp.bfloat16)
        f32 = jnp.float32
        keep = functools.partial(pltpu.with_memory_space_constraint, memory_space=pltpu.HBM)
        new_weights, new_basis, new_momentum = pl.pallas_call(
            functools.partial(kernel, ndp, ntp),
            out_shape=(
                jax.ShapeDtypeStruct((layers, columns, rows), f32),
                jax.ShapeDtypeStruct((layers, rank, width), f32),
                jax.ShapeDtypeStruct((layers, columns, rows), f32),
            ),
            in_specs=[
                pl.BlockSpec(memory_space=pltpu.HBM),
                pl.BlockSpec(memory_space=pltpu.VMEM),
                pl.BlockSpec(memory_space=pltpu.HBM),
                pl.BlockSpec(memory_space=pltpu.HBM),
            ],
            out_specs=[pl.BlockSpec(memory_space=pltpu.VMEM)] * 3,
            scratch_shapes=[
                pltpu.VMEM((layers, rows, width), jnp.bfloat16),
                pltpu.VMEM((layers, columns, rows), f32),
                pltpu.VMEM((layers, columns, rows), f32),
                pltpu.VMEM((layers, ndp, rank, rows), f32),
                pltpu.VMEM((ntp, rank, LANES), f32),
                pltpu.VMEM((pieces, rank, LANES), f32),
                pltpu.VMEM((rounds, n, rank, LANES), f32),
                pltpu.VMEM((pieces, rank, LANES), f32),
                pltpu.VMEM((layers, 6 * rank, rows), jnp.bfloat16),
                pltpu.SemaphoreType.DMA((layers,)),
                pltpu.SemaphoreType.DMA((2,)),
                pltpu.SemaphoreType.DMA,
                pltpu.SemaphoreType.DMA((layers,)),
                pltpu.SemaphoreType.DMA,
                pltpu.SemaphoreType.DMA,
                pltpu.SemaphoreType.DMA,
                pltpu.SemaphoreType.DMA((rounds,)),
                pltpu.SemaphoreType.DMA,
                pltpu.SemaphoreType.DMA((pieces,)),
            ],
            compiler_params=pltpu.CompilerParams(
                collective_id=0, has_side_effects=True, vmem_limit_bytes=24 * 1024 * 1024
            ),
        )(
            keep(gradients[0]), basis,
            keep(jnp.swapaxes(weights_before, 1, 2)), keep(jnp.swapaxes(momentum, 1, 2)),
        )
        return tuple(jnp.swapaxes(x, 1, 2) for x in (new_weights, new_basis, new_momentum))

    in_specs = (P("dp", None, "tp", None), P(), P(None, "tp", "dp"), P(None, "tp", "dp"))
    out_specs = (P(None, "tp", "dp"), P(), P(None, "tp", "dp"))
    return jax.shard_map(on_device, mesh=mesh, in_specs=in_specs, out_specs=out_specs, check_vma=False)
```

time: 171 us -> 26.3 us (0.15)
  waiting for transfers between devices: 80.7 us -> 0 us
  blocking collectives: 57.7 us -> 0 us
  Pallas kernels: 0 us -> 22 us
  between operations: 14.1 us -> 0.64 us
  matrix products: 8.45 us -> 0 us
  other arithmetic: 7.59 us -> 0.9 us
    psum x1 -> x0, waiting for transfers between devices: 80.7 us -> none  [on_device(): right, gram = lax.psum((part_right, own_share), ('dp', 'tp'))]
    psum x2 -> x0, blocking collectives: 57.7 us -> none  [the longest x1 39.5 us: on_device(): right, gram = lax.psum((part_right, own_share), ('dp', 'tp'))]
    pallas_call x0 -> x1, Pallas kernels: none -> 22 us  [on_device(): pl.pallas_call(functools.partial(kernel, ndp, ntp), out_shape=(jax.ShapeD...]
    dot_general x4 -> x0, matrix products: 7.23 us -> none  [the longest x1 4.38 us: on_device(): jnp.einsum('lir,lrw->liw', left, mixed, precision=lax.Precision.HIGHEST)]
    another operation x7 -> x0, other arithmetic: 5.67 us -> none  [the longest x4 3.08 us: on_device(): root = jnp.linalg.cholesky(gram)]
  transfers between devices with their start and end apart: 1 -> 0, of which waited for: 1 -> 0; matrix products, arithmetic and copies ran while one was open for 4% -> 0% of each run, Pallas kernels for 0% -> 0%
where the time goes in v1:
time: 26.3 us; the launch traced here: 26.2 us
  Pallas kernels  22 us (84%)
  local copies, waits for them, and re-layouts  2.67 us (10%)
  other arithmetic  0.9 us (3%)
  between operations  0.64 us (2%)
    pallas_call x1, Pallas kernels, on_device(): pl.pallas_call(functools.partial(kernel, ndp, ntp), out_shape=(jax.ShapeD...  22 us
    unnamed x3, local copies, waits for them, and re-layouts  2.67 us
    convert_element_type x1, other arithmetic, on_device(): basis = jnp.swapaxes(right_factor, 1, 2).astype(jnp.bfloat16)  0.9 us

profile of v1, /device:TPU:0, one launch (start us, length us, event | category | flops | bytes accessed | tf_op | source)
XLA Modules:
  0.0 26.2 jit_solution(192467688640423687)
XLA Ops:
  0.6 0.9 %convert_bitcast_fusion.basis = bf16[4,8,768]{2,1,0:T(8,128)(2,1)S(1)} fusion(f32[4,768,8]{1,2,0:T(8,128)} %param.5), kind=kLoop, calls=%fused_computation | loop fusion | flops 24576 | bytes 147456 | tf_op jit(solution)/shard_map/convert_element_type | solution.py:215
  1.5 22.0 %shard_map.67 = (f32[4,192,384]{2,1,0:T(8,128)S(1)}, f32[4,8,768]{2,1,0:T(8,128)S(1)}, f32[4,192,384]{2,1,0:T(8,128)S(1)}) custom-call(bf16[4,384,768]{2,1,0:T(8,128)(2,1)} %bitcast.11, bf16[4,8,768]{2,1,0:T(8,128)(2,1)S(1)} %convert_bitcast_fusion.basis, f32[4,192,384]{2,1,0:T(8,128)} %bitcast.12, f32[4,192,384]{2,1,0:T(8,128)} %bitcast.13), custom_call_target="tpu_custom_call" | custom-call | tf_op jit(solution)/shard_map/pallas_call | solution.py:218
  23.5 1.0 %copy.10 = f32[4,384,192]{1,2,0:T(8,128)} copy(f32[4,384,192]{1,2,0:T(8,128)S(1)} %bitcast.9) | data formatting | bytes 2359296
  24.6 0.6 %copy.11 = f32[4,768,8]{1,2,0:T(8,128)} copy(f32[4,768,8]{1,2,0:T(8,128)S(1)} %bitcast.10) | data formatting | bytes 196608
  25.2 1.0 %copy.12 = f32[4,384,192]{1,2,0:T(8,128)} copy(f32[4,384,192]{1,2,0:T(8,128)S(1)} %bitcast.8) | data formatting | bytes 2359296

commit v2 on v1

--- a/solution.py
+++ b/solution.py
@@ -22,7 +22,7 @@
 def kernel(
     ndp, ntp, grads, basis, weights, momentum,
     out_weights, out_basis, out_momentum,
-    g_buf, w_buf, m_buf, lefts, grams, rights, parts, full, y_buf,
+    b_buf, g_buf, w_buf, m_buf, lefts, grams, rights, parts, full, y_buf,
     g_sem, wm_sem, left_send, left_recv, gram_send, gram_recv, part_send, part_recv, full_send, full_recv,
 ):
     layers, rank, rows = lefts.shape[0], lefts.shape[2], lefts.shape[3]
@@ -34,12 +34,31 @@
     my_dp, my_tp = lax.axis_index("dp"), lax.axis_index("tp")
     me = my_dp * ntp + my_tp
 
+    group = -(-pieces // ndp)
+    span = max(
+        ((d + 1) * columns - 1) // LANES - d * columns // LANES + 1 for d in range(ndp)
+    )
+
     def device(flat):
         return (flat // ntp, lax.rem(flat, ntp))
+
+    def owner_of(l, t):
+        place = t * layers + l
+        within = place % group
+        tp = within * ntp // group if group <= ntp else within % ntp
+        return place // group * ntp + tp
+
+    def round_of(l, t):
+        return 0 if group <= ntp else (t * layers + l) % group // ntp
+
+    def first_tile(d, least=min):
+        return least(d * columns // LANES, tiles - span)
 
     loads = [pltpu.make_async_copy(grads.at[l], g_buf.at[l], g_sem.at[l]) for l in range(layers)]
     for load in loads:
         load.start()
+    basis_load = pltpu.make_async_copy(basis, b_buf, wm_sem.at[2])
+    basis_load.start()
     state_loads = [
         pltpu.make_async_copy(weights, w_buf, wm_sem.at[0]),
         pltpu.make_async_copy(momentum, m_buf, wm_sem.at[1]),
@@ -60,20 +79,22 @@
         )
 
     for l in range(layers):
+        if l == 0:
+            basis_load.wait()
         loads[l].wait()
         lefts[l, my_dp] = lax.dot_general(
-            basis[l], g_buf[l], (((1,), (1,)), ((), ())), preferred_element_type=jnp.float32
+            b_buf[l].astype(jnp.bfloat16), g_buf[l], (((1,), (1,)), ((), ())), preferred_element_type=jnp.float32
         )
         if l == 0:
             pl.semaphore_wait(barrier, n - 1)
         for k in range(1, ndp):
             left_copy(l, k).start()
 
-    def part_copy(j):
-        owner = j % n
+    def part_copy(l, t):
+        j, owner, turn = l * tiles + t, owner_of(l, t), round_of(l, t)
         return pltpu.make_async_remote_copy(
-            src_ref=rights.at[j], dst_ref=parts.at[j // n, me],
-            send_sem=part_send, recv_sem=part_recv.at[j // n],
+            src_ref=rights.at[j], dst_ref=parts.at[turn, me],
+            send_sem=part_send, recv_sem=part_recv.at[turn],
             device_id=(owner // ntp, owner % ntp), device_id_type=MESH,
         )
 
@@ -90,11 +111,10 @@
         for t in range(tiles):
             rights[l * tiles + t] = right[:, t * LANES:(t + 1) * LANES]
         for t in range(tiles):
-            j = l * tiles + t
-
-            @pl.when(me != j % n)
+
+            @pl.when(me != owner_of(l, t))
             def _():
-                part_copy(j).start()
+                part_copy(l, t).start()
 
     stacked = jnp.concatenate(all_left, axis=0)
     products = lax.dot_general(
@@ -117,24 +137,32 @@
     for k in range(1, ntp):
         gram_copy(k).start()
 
-    def full_copy(j, k):
-        return pltpu.make_async_remote_copy(
-            src_ref=full.at[j], dst_ref=full.at[j],
-            send_sem=full_send, recv_sem=full_recv.at[j],
-            device_id=device(lax.rem(me + k, n)), device_id_type=MESH,
-        )
-
-    for j in range(pieces):
-        q = j // n
-
-        @pl.when(me == j % n)
+    every = [(l, t) for l in range(layers) for t in range(tiles)]
+
+    def full_copies(l, t):
+        j, owner = l * tiles + t, owner_of(l, t)
+        others = [(d, p) for d in range(ndp) for p in range(ntp) if d * ntp + p != owner]
+        others.sort(key=lambda x: (not 0 <= t - first_tile(x[0]) < span, -abs(x[1] - owner % ntp)))
+        return [
+            pltpu.make_async_remote_copy(
+                src_ref=full.at[j], dst_ref=full.at[j],
+                send_sem=full_send, recv_sem=full_recv.at[j],
+                device_id=other, device_id_type=MESH,
+            )
+            for other in others
+        ]
+
+    for l, t in every:
+        q, j = round_of(l, t), l * tiles + t
+
+        @pl.when(me == owner_of(l, t))
         def _():
             landed = parts.at[q, pl.ds(0, n - 1)]
             pltpu.make_async_copy(landed, landed, part_recv.at[q]).wait()
             parts[q, me] = rights[j]
             full[j] = jnp.sum(parts[q], axis=0)
-            for k in range(1, n):
-                full_copy(j, k).start()
+            for copy in full_copies(l, t):
+                copy.start()
 
     if ntp > 1:
         landed = grams.at[pl.ds(0, ntp - 1)]
@@ -167,22 +195,34 @@
     for load in state_loads:
         load.wait()
 
-    shift = lax.rem(width - my_dp * columns, width)
-    for l in range(layers):
-        for t in range(tiles):
-            j = l * tiles + t
-
-            @pl.when(me != j % n)
+    def wait_full(j):
+        pltpu.make_async_copy(full.at[j], full.at[j], full_recv.at[j]).wait()
+
+    start = first_tile(my_dp, jnp.minimum)
+    shift = lax.rem(span * LANES - (my_dp * columns - start * LANES), span * LANES)
+    for l in range(layers):
+        for i in range(span):
+            t = start + i
+
+            @pl.when(me != owner_of(l, t))
             def _():
-                pltpu.make_async_copy(full.at[j], full.at[j], full_recv.at[j]).wait()
-        right = jnp.concatenate([full[l * tiles + t] for t in range(tiles)], axis=1)
-        own = pltpu.roll(right, shift, 1)[:, :columns]
+                wait_full(l * tiles + t)
+        near = jnp.concatenate([full[l * tiles + start + i] for i in range(span)], axis=1)
+        own = pltpu.roll(near, shift, 1)[:, :columns]
         high, mid, low = split3(own)
         own = jnp.concatenate([high, mid, low, high, mid, high], axis=0).T.astype(jnp.bfloat16)
         change = jnp.dot(own, y_buf[l], preferred_element_type=jnp.float32) / ndp
         moved = 0.9 * m_buf[l] + change
         out_momentum[l] = moved
         out_weights[l] = w_buf[l] - 0.02 * moved
+
+    for l in range(layers):
+        for t in range(tiles):
+
+            @pl.when((me != owner_of(l, t)) & ((t < start) | (t >= start + span)))
+            def _():
+                wait_full(l * tiles + t)
+        right = jnp.concatenate([full[l * tiles + t] for t in range(tiles)], axis=1)
         out_basis[l] = right * lax.rsqrt(jnp.mean(right * right) + 1e-12)
 
     for l in range(layers):
@@ -190,16 +230,16 @@
             left_copy(l, k).wait_send()
     for k in range(1, ntp):
         gram_copy(k).wait_send()
-    for j in range(pieces):
-
-        @pl.when(me != j % n)
+    for l, t in every:
+
+        @pl.when(me != owner_of(l, t))
         def _():
-            part_copy(j).wait_send()
-
-        @pl.when(me == j % n)
+            part_copy(l, t).wait_send()
+
+        @pl.when(me == owner_of(l, t))
         def _():
-            for k in range(1, n):
-                full_copy(j, k).wait_send()
+            for copy in full_copies(l, t):
+                copy.wait_send()
 
 
 def solution(mesh):
@@ -211,8 +251,8 @@
         rank = right_factor.shape[2]
         columns = weights_before.shape[2]
         pieces = layers * (width // LANES)
-        rounds = -(-pieces // n)
-        basis = jnp.swapaxes(right_factor, 1, 2).astype(jnp.bfloat16)
+        rounds = -(-(-(-pieces // ndp)) // ntp)
+        basis = jnp.swapaxes(right_factor, 1, 2)
         f32 = jnp.float32
         keep = functools.partial(pltpu.with_memory_space_constraint, memory_space=pltpu.HBM)
         new_weights, new_basis, new_momentum = pl.pallas_call(
@@ -224,12 +264,13 @@
             ),
             in_specs=[
                 pl.BlockSpec(memory_space=pltpu.HBM),
-                pl.BlockSpec(memory_space=pltpu.VMEM),
+                pl.BlockSpec(memory_space=pltpu.HBM),
                 pl.BlockSpec(memory_space=pltpu.HBM),
                 pl.BlockSpec(memory_space=pltpu.HBM),
             ],
             out_specs=[pl.BlockSpec(memory_space=pltpu.VMEM)] * 3,
             scratch_shapes=[
+                pltpu.VMEM((layers, rank, width), f32),
                 pltpu.VMEM((layers, rows, width), jnp.bfloat16),
                 pltpu.VMEM((layers, columns, rows), f32),
                 pltpu.VMEM((layers, columns, rows), f32),
@@ -240,7 +281,7 @@
                 pltpu.VMEM((pieces, rank, LANES), f32),
                 pltpu.VMEM((layers, 6 * rank, rows), jnp.bfloat16),
                 pltpu.SemaphoreType.DMA((layers,)),
-                pltpu.SemaphoreType.DMA((2,)),
+                pltpu.SemaphoreType.DMA((3,)),
                 pltpu.SemaphoreType.DMA,
                 pltpu.SemaphoreType.DMA((layers,)),
                 pltpu.SemaphoreType.DMA,
@@ -254,7 +295,7 @@
                 collective_id=0, has_side_effects=True, vmem_limit_bytes=24 * 1024 * 1024
             ),
         )(
-            keep(gradients[0]), basis,
+            keep(gradients[0]), keep(basis),
             keep(jnp.swapaxes(weights_before, 1, 2)), keep(jnp.swapaxes(momentum, 1, 2)),
         )
         return tuple(jnp.swapaxes(x, 1, 2) for x in (new_weights, new_basis, new_momentum))

time: 26.3 us -> 24.9 us (0.947)
  other arithmetic: 0.9 us -> 0 us
  Pallas kernels: 22 us -> 21.4 us
    convert_element_type x1 -> x0, other arithmetic: 0.9 us -> none  [on_device(): basis = jnp.swapaxes(right_factor, 1, 2).astype(jnp.bfloat16)]
    pallas_call x1, Pallas kernels: 22 us -> 21.4 us  [on_device(): pl.pallas_call(functools.partial(kernel, ndp, ntp), out_shape=(jax.ShapeD...]
where the time goes in v2:
time: 24.9 us; the launch traced here: 24.7 us
  Pallas kernels  21.4 us (86%)
  local copies, waits for them, and re-layouts  2.67 us (11%)
  between operations  0.64 us (3%)
    pallas_call x1, Pallas kernels, on_device(): pl.pallas_call(functools.partial(kernel, ndp, ntp), out_shape=(jax.ShapeD...  21.4 us
    unnamed x3, local copies, waits for them, and re-layouts  2.67 us

profile of v2, /device:TPU:0, one launch (start us, length us, event | category | flops | bytes accessed | tf_op | source)
XLA Modules:
  0.0 24.7 jit_solution(17187269823702961425)
XLA Ops:
  0.6 21.4 %shard_map.67 = (f32[4,192,384]{2,1,0:T(8,128)S(1)}, f32[4,8,768]{2,1,0:T(8,128)S(1)}, f32[4,192,384]{2,1,0:T(8,128)S(1)}) custom-call(bf16[4,384,768]{2,1,0:T(8,128)(2,1)} %bitcast.10, f32[4,8,768]{2,1,0:T(8,128)} %bitcast.13, f32[4,192,384]{2,1,0:T(8,128)} %bitcast.11, f32[4,192,384]{2,1,0:T(8,128)} %bitcast.12), custom_call_target="tpu_custom_call" | custom-call | tf_op jit(solution)/shard_map/pallas_call | solution.py:258
  22.1 1.0 %copy.10 = f32[4,384,192]{1,2,0:T(8,128)} copy(f32[4,384,192]{1,2,0:T(8,128)S(1)} %bitcast.8) | data formatting | bytes 2359296
  23.1 0.6 %copy.11 = f32[4,768,8]{1,2,0:T(8,128)} copy(f32[4,768,8]{1,2,0:T(8,128)S(1)} %bitcast.9) | data formatting | bytes 196608
  23.7 1.0 %copy.12 = f32[4,384,192]{1,2,0:T(8,128)} copy(f32[4,384,192]{1,2,0:T(8,128)S(1)} %bitcast.7) | data formatting | bytes 2359296
